TPU v7x, 16 devices: a whole 2x2x2 slice. The times are simulated.
16 devices in a mesh: req: 4 (over z, y), dap: 4 (over x, core).
Axes of the slice: x: 2, y: 2, z: 2, core: 2. Of those that a mesh axis runs over, the one named last changes fastest.
Arguments:
- msa_act: bfloat16 [256, 256, 256], P(('req', 'dap')), parts along dimension 0
- pair_act: bfloat16 [1024, 256, 128], P(('req', 'dap')), parts along dimension 0
- msa_mask: int32 [256, 256], P(('req', 'dap')), parts along dimension 0
- pair_mask: int32 [1024, 256], P(('req', 'dap')), parts along dimension 0
- row_qkvg: bfloat16 [2, 256, 1024], replicated
- row_bias: bfloat16 [2, 128, 8], replicated
- row_out: bfloat16 [2, 256, 256], replicated
- col_qkvg: bfloat16 [2, 256, 1024], replicated
- col_out: bfloat16 [2, 256, 256], replicated
- mtr_in: bfloat16 [2, 256, 1024], replicated
- mtr_out: bfloat16 [2, 1024, 256], replicated
- opm_proj: bfloat16 [2, 256, 64], replicated
- opm_out: bfloat16 [2, 1024, 128], replicated
- tmo_proj: bfloat16 [2, 128, 640], replicated
- tmo_out: bfloat16 [2, 128, 128], replicated
- tmi_proj: bfloat16 [2, 128, 640], replicated
- tmi_out: bfloat16 [2, 128, 128], replicated
- tas_qkvg: bfloat16 [2, 128, 512], replicated
- tas_bias: bfloat16 [2, 128, 4], replicated
- tas_out: bfloat16 [2, 128, 128], replicated
- tae_qkvg: bfloat16 [2, 128, 512], replicated
- tae_bias: bfloat16 [2, 128, 4], replicated
- tae_out: bfloat16 [2, 128, 128], replicated
- ptr_in: bfloat16 [2, 128, 512], replicated
- ptr_out: bfloat16 [2, 512, 128], replicated
Outputs:
- output 1: bfloat16 [256, 256, 256], P(('req', 'dap')), parts along dimension 0
- output 2: bfloat16 [1024, 256, 128], P(('req', 'dap')), parts along dimension 0
There are 4 independent parts. A program takes and returns all parts, laid end to end along the dimension named above; an argument that names none is the same for every part.
All inputs are finite; a program needn't handle non-finite values.
Results may differ from a plain program's by a relative error of at most 0.02.
Values are sent between devices in bfloat16 or wider.
A program may use at most 1 GiB of HBM per device.

v0:
```python
import jax
import jax.numpy as jnp
from jax import lax
from jax.sharding import PartitionSpec as P

GROUP_AXIS = 'dap'
PARTS_AXIS = 'req'
MASKED_LOGIT = -1e9


def layer_norm(x):
    values = x.astype(jnp.float32)
    centered = values - jnp.mean(values, axis=-1, keepdims=True)
    variance = jnp.mean(centered * centered, axis=-1, keepdims=True)
    return (centered * lax.rsqrt(variance + 1e-5)).astype(jnp.bfloat16)


def residual(x, update):
    return (x.astype(jnp.float32) + update).astype(jnp.bfloat16)


def dense(x, weight):
    return jnp.einsum('...c,cf->...f', x, weight, preferred_element_type=jnp.float32)


def attend(queries, gate_raw, keyvals, num_heads, pair_bias, key_mask, w_out):
    n_batch, q_len, head_width = queries.shape
    k_len = keyvals.shape[1]
    head_dim = head_width // num_heads
    q_heads = queries.reshape(n_batch, q_len, num_heads, head_dim)
    k_heads = keyvals[..., :head_width].reshape(n_batch, k_len, num_heads, head_dim)
    v_heads = keyvals[..., head_width:].reshape(n_batch, k_len, num_heads, head_dim)
    logits = jnp.einsum('bqhd,bkhd->bhqk', q_heads, k_heads, preferred_element_type=jnp.float32) * head_dim ** -0.5
    if pair_bias is not None:
        logits = logits + pair_bias.astype(jnp.float32)
    logits = jnp.where(key_mask[:, None, None, :] > 0, logits, MASKED_LOGIT)
    attn_prob = jax.nn.softmax(logits, axis=-1).astype(jnp.bfloat16)
    attended = jnp.einsum('bhqk,bkhd->bqhd', attn_prob, v_heads, preferred_element_type=jnp.float32)
    gated = (attended.reshape(n_batch, q_len, head_width) * jax.nn.sigmoid(gate_raw.astype(jnp.float32))).astype(jnp.bfloat16)
    return dense(gated, w_out)


def self_attention(x_norm, w_qkvg, num_heads, pair_bias, key_mask, w_out):
    head_width = w_out.shape[0]
    projected = dense(x_norm, w_qkvg).astype(jnp.bfloat16)
    return attend(projected[..., :head_width], projected[..., 3 * head_width:], projected[..., head_width:3 * head_width], num_heads, pair_bias, key_mask, w_out)


def head_bias(pair_norm, w_bias):
    return jnp.einsum('ijc,ch->hij', pair_norm, w_bias, preferred_element_type=jnp.float32).astype(jnp.bfloat16)


def transition(x, w_in, w_out):
    hidden = jnp.maximum(dense(layer_norm(x), w_in), 0.0).astype(jnp.bfloat16)
    return dense(hidden, w_out)


def outer_update(array_b7, res_mask, full_mask, w_proj, w_out):
    opm_dim = w_proj.shape[1] // 2
    projected = dense(layer_norm(array_b7), w_proj).astype(jnp.bfloat16)
    mask_bf = res_mask.astype(jnp.bfloat16)[:, :, None]
    left_act = projected[..., :opm_dim] * mask_bf
    right_act = projected[..., opm_dim:] * mask_bf
    right_full = lax.all_gather(right_act, GROUP_AXIS, axis=1, tiled=True)
    outer_prod = jnp.einsum('sic,sje->ijce', left_act, right_full, preferred_element_type=jnp.float32).astype(jnp.bfloat16)
    n_rows, n_cols = outer_prod.shape[:2]
    update = dense(outer_prod.reshape(n_rows, n_cols, opm_dim * opm_dim), w_out)
    overlap = jnp.einsum('si,sj->ij', res_mask.astype(jnp.float32), full_mask.astype(jnp.float32))
    return update / (1e-3 + overlap)[:, :, None]


def tri_gates(pair_rows, mask_rows, w_proj):
    tri_dim = (w_proj.shape[1] - pair_rows.shape[-1]) // 4
    projected = dense(layer_norm(pair_rows), w_proj)
    mask_f = mask_rows.astype(jnp.float32)[:, :, None]
    left_act = (mask_f * jax.nn.sigmoid(projected[..., 2 * tri_dim:3 * tri_dim]) * projected[..., :tri_dim]).astype(jnp.bfloat16)
    right_act = (mask_f * jax.nn.sigmoid(projected[..., 3 * tri_dim:4 * tri_dim]) * projected[..., tri_dim:2 * tri_dim]).astype(jnp.bfloat16)
    gate_act = jax.nn.sigmoid(projected[..., 4 * tri_dim:])
    return left_act, right_act, gate_act


def tri_finish(product, gate_act, w_out):
    return gate_act * dense(layer_norm(product), w_out)


def tri_attention(pair_rows, mask_rows, w_qkvg, w_bias, w_out):
    pair_norm = layer_norm(pair_rows)
    bias_full = lax.all_gather(head_bias(pair_norm, w_bias), GROUP_AXIS, axis=1, tiled=True)
    return self_attention(pair_norm, w_qkvg, w_bias.shape[1], bias_full, mask_rows, w_out)


def pair_stack(pair_loc, pair_mask, pair_mask_t, pair_w):
    (tmo_proj, tmo_out, tmi_proj, tmi_out, tas_qkvg, tas_bias, tas_out,
     tae_qkvg, tae_bias, tae_out, ptr_in, ptr_out) = pair_w
    left_act, right_act, gate_act = tri_gates(pair_loc, pair_mask, tmo_proj)
    right_full = lax.all_gather(right_act, GROUP_AXIS, axis=0, tiled=True)
    product = jnp.einsum('ikc,jkc->ijc', left_act, right_full, preferred_element_type=jnp.float32)
    pair_loc = residual(pair_loc, tri_finish(product, gate_act, tmo_out))
    left_act, right_act, gate_act = tri_gates(pair_loc, pair_mask, tmi_proj)
    left_cols = lax.all_to_all(left_act, GROUP_AXIS, 1, 0, tiled=True)
    right_full = lax.all_gather(right_act, GROUP_AXIS, axis=0, tiled=True)
    product = jnp.einsum('kic,kjc->ijc', left_cols, right_full, preferred_element_type=jnp.float32)
    pair_loc = residual(pair_loc, tri_finish(product, gate_act, tmi_out))
    pair_loc = residual(pair_loc, tri_attention(pair_loc, pair_mask, tas_qkvg, tas_bias, tas_out))
    pair_cols = lax.all_to_all(pair_loc, GROUP_AXIS, 1, 0, tiled=True)
    pair_t = jnp.swapaxes(pair_cols, 0, 1)
    pair_t = residual(pair_t, tri_attention(pair_t, pair_mask_t, tae_qkvg, tae_bias, tae_out))
    pair_loc = lax.all_to_all(jnp.swapaxes(pair_t, 0, 1), GROUP_AXIS, 0, 1, tiled=True)
    return residual(pair_loc, transition(pair_loc, ptr_in, ptr_out))


def evoformer_block(value_a7, pair_loc, full_mask, full_pair_mask, layer_w):
    (row_qkvg, row_bias, row_out, col_qkvg, col_out, mtr_in, mtr_out, opm_proj, opm_out) = layer_w[:9]
    shard_idx = lax.axis_index(GROUP_AXIS)
    seq_loc = value_a7.shape[0]
    res_loc = pair_loc.shape[0]
    seq_mask = lax.dynamic_slice_in_dim(full_mask, shard_idx * seq_loc, seq_loc, 0)
    res_mask = lax.dynamic_slice_in_dim(full_mask, shard_idx * res_loc, res_loc, 1)
    pair_mask = lax.dynamic_slice_in_dim(full_pair_mask, shard_idx * res_loc, res_loc, 0)
    pair_mask_t = lax.dynamic_slice_in_dim(full_pair_mask, shard_idx * res_loc, res_loc, 1).T
    value_a9 = row_bias.shape[1]
    row_bias_full = lax.all_gather(head_bias(layer_norm(pair_loc), row_bias), GROUP_AXIS, axis=1, tiled=True)
    value_a7 = residual(value_a7, self_attention(layer_norm(value_a7), row_qkvg, value_a9, row_bias_full, seq_mask, row_out))
    array_b7 = lax.all_to_all(value_a7, GROUP_AXIS, 1, 0, tiled=True)
    col_norm = jnp.swapaxes(layer_norm(array_b7), 0, 1)
    col_update = self_attention(col_norm, col_qkvg, value_a9, None, res_mask.T, col_out)
    array_b7 = residual(array_b7, jnp.swapaxes(col_update, 0, 1))
    array_b7 = residual(array_b7, transition(array_b7, mtr_in, mtr_out))
    pair_loc = residual(pair_loc, outer_update(array_b7, res_mask, full_mask, opm_proj, opm_out))
    pair_loc = pair_stack(pair_loc, pair_mask, pair_mask_t, layer_w[9:])
    value_a7 = lax.all_to_all(array_b7, GROUP_AXIS, 0, 1, tiled=True)
    return value_a7, pair_loc


def solution(mesh):
    row_spec = P((PARTS_AXIS, GROUP_AXIS))

    def local_body(value_a7, pair_loc, value_a12, pair_mask_loc, *weights):
        full_mask = lax.all_gather(value_a12, GROUP_AXIS, axis=0, tiled=True)
        full_pair_mask = lax.all_gather(pair_mask_loc, GROUP_AXIS, axis=0, tiled=True)
        for layer_idx in range(weights[0].shape[0]):
            layer_w = tuple(weight[layer_idx] for weight in weights)
            value_a7, pair_loc = evoformer_block(value_a7, pair_loc, full_mask, full_pair_mask, layer_w)
        return value_a7, pair_loc

    def run_blocks(*arrays):
        n_weights = len(arrays) - 4
        return jax.shard_map(local_body, mesh=mesh, in_specs=(row_spec,) * 4 + (P(),) * n_weights, out_specs=(row_spec, row_spec), check_vma=False)(*arrays)

    return run_blocks
```

profile of v0, /device:TPU:0, one launch (start us, length us, event | category | flops | bytes accessed | tf_op | source)
XLA Modules:
  0.0 2247.1 jit_solution(15341350923280030578)
XLA Ops:
  51.7 18.7 fusion.452
  70.4 16.2 fusion.46
  102.7 25.3 %all-to-all-done = bf16[16,256,256]{2,0,1:T(8,128)(2,1)S(1)} async-done(((bf16[16,256,256]{2,0,1:T(8,128)(2,1)}), bf16[16,256,256]{2,0,1:T(8,128)(2,1)S(1)}, u32[]{:S(2)}, u32[]{:S(2)}) %all-to-all-start) | async-done | bytes 2097184 | tf_op jit(solution)/shard_map/all_to_all | solution.py:124
  163.0 14.1 fusion.453
  232.3 14.3 all-gather.11.cloned.1.call-done
  246.6 15.6 convert_bitcast_fusion.1
  262.3 31.3 %copy.595 = bf16[64,256,32,32]{1,3,2,0:T(8,128)(2,1)} copy(bf16[64,256,32,32]{1,0,2,3:T(8,128)(2,1)} %convert_bitcast_fusion.1) | data formatting | bytes 67108864 | tf_op jit(solution)/shard_map/convert_element_type | solution.py:65
  293.6 14.6 convert_reduce_fusion.6
  309.9 16.4 fusion.204
  326.3 17.3 fusion.144
  350.1 105.2 %all-gather.13.cloned.1.call-done = bf16[256,256,128]{2,1,0:T(8,128)(2,1)} async-done(((bf16[64,256,128]{2,1,0:T(8,128)(2,1)}), bf16[256,256,128]{2,1,0:T(8,128)(2,1)}) %all-gather.13.cloned.1.call-update) | async-done | bytes 16777232 | tf_op jit(solution)/shard_map/all_gather | solution.py:96
  455.3 21.8 copy.605
  509.1 16.5 fusion.206
  525.7 16.9 fusion.130
  561.2 92.3 %all-to-all-done.2 = bf16[64,256,128]{2,0,1:T(8,128)(2,1)} async-done(((bf16[64,256,128]{2,0,1:T(8,128)(2,1)}), bf16[64,256,128]{2,0,1:T(8,128)(2,1)}, u32[]{:S(2)}, u32[]{:S(2)}) %all-to-all-start.2) | async-done | bytes 4194336 | tf_op jit(solution)/shard_map/all_to_all | solution.py:100
  667.8 31.4 %all-gather.15.cloned.1.call-done = bf16[256,256,128]{2,1,0:T(8,128)(2,1)} async-done(((bf16[64,256,128]{2,1,0:T(8,128)(2,1)}), bf16[256,256,128]{2,1,0:T(8,128)(2,1)}) %all-gather.15.cloned.1.call-update) | async-done | bytes 16777232 | tf_op jit(solution)/shard_map/all_gather | solution.py:101
  699.2 21.8 copy.619
  771.9 31.9 %fusion.454 = (f32[64,4,256]{2,1,0:T(4,128)S(1)}, f32[64,4,256,256]{2,3,1,0:T(8,128)}) fusion(f32[4,256,256]{1,2,0:T(8,128)S(1)} %copy.627, pred[64,256]{1,0:T(8,128)(4,1)S(1)} %dynamic-slice_compare_fusion.1, bf16[64,256,4,32]{1,3,2,0:T(8,128)(2,1)} %bitcast.560, bf16[64,256,4,32]{1,3,2,0:T(8,128)(2,1)} %bitcast.559), kind=kOutput, calls=%fused_computation.618 | convolution fusion | flops 1157628160 | bytes 76824576 | tf_op jit(solution)/shard_map/sub | solution.py:37
  803.7 26.4 %fusion.28 = f32[64,4,32,256]{3,2,1,0:T(8,128)} fusion(bf16[64,256,4,32]{1,3,2,0:T(8,128)(2,1)} %bitcast.556, f32[64,4,256,256]{2,3,1,0:T(8,128)} %get-tuple-element.59, f32[64,4,256]{2,1,0:T(4,128)S(1)} %get-tuple-element.58), kind=kOutput, calls=%fused_computation.50 | convolution fusion | flops 1107296256 | bytes 79953920 | tf_op jit(solution)/shard_map/bhqk,bkhd->bqhd/dot_general | solution.py:38
  854.3 45.1 %all-to-all-done.3 = bf16[64,256,128]{2,0,1:T(8,128)(2,1)} async-done(((bf16[64,256,128]{2,0,1:T(8,128)(2,1)}), bf16[64,256,128]{2,0,1:T(8,128)(2,1)}, u32[]{:S(2)}, u32[]{:S(2)}) %all-to-all-start.3) | async-done | bytes 4194336 | tf_op jit(solution)/shard_map/all_to_all | solution.py:105
  954.9 31.9 %fusion.455 = (f32[64,4,256]{2,1,0:T(4,128)S(1)}, f32[64,4,256,256]{2,3,1,0:T(8,128)}) fusion(f32[4,256,256]{1,2,0:T(8,128)S(1)} %copy.637, pred[64,256]{1,0:T(8,128)(4,1)S(1)} %copy.635, bf16[64,256,4,32]{1,3,2,0:T(8,128)(2,1)} %bitcast.552, bf16[64,256,4,32]{1,3,2,0:T(8,128)(2,1)} %bitcast.551), kind=kOutput, calls=%fused_computation.619 | convolution fusion | flops 1157628160 | bytes 76824576 | tf_op jit(solution)/shard_map/sub | solution.py:37
  986.7 26.4 %fusion.29 = f32[64,4,32,256]{3,2,1,0:T(8,128)} fusion(bf16[64,256,4,32]{1,3,2,0:T(8,128)(2,1)} %bitcast.549, f32[64,4,256,256]{2,3,1,0:T(8,128)} %get-tuple-element.61, f32[64,4,256]{2,1,0:T(4,128)S(1)} %get-tuple-element.60), kind=kOutput, calls=%fused_computation.51 | convolution fusion | flops 1107296256 | bytes 79953920 | tf_op jit(solution)/shard_map/bhqk,bkhd->bqhd/dot_general | solution.py:38
  1038.1 43.0 %all-to-all-done.4 = bf16[256,64,128]{2,1,0:T(8,128)(2,1)} async-done(((bf16[256,64,128]{2,1,0:T(8,128)(2,1)}), bf16[256,64,128]{2,1,0:T(8,128)(2,1)}, u32[]{:S(2)}, u32[]{:S(2)}) %all-to-all-start.4) | async-done | bytes 4194336 | tf_op jit(solution)/shard_map/all_to_all | solution.py:108
  1118.4 14.2 convert_reduce_fusion.3
  1167.3 20.5 fusion.458
  1187.8 16.2 fusion.47
  1216.1 28.1 %all_to_all.117 = bf16[16,256,256]{2,0,1:T(8,128)(2,1)S(1)} all-to-all(bf16[16,256,256]{2,0,1:T(8,128)(2,1)S(1)} %copy.649), channel_id=1, replica_groups=mesh['req'=4,'dap'=4] {'dap'}, dimensions={1} | all-to-all | bytes 4194304 | tf_op jit(solution)/shard_map/all_to_all | solution.py:124
  1280.2 13.9 fusion.459
  1343.7 19.9 all-gather.19.cloned.1.call-done
  1363.6 15.5 convert_bitcast_fusion
  1379.1 31.4 %copy.670 = bf16[64,256,32,32]{1,3,2,0:T(8,128)(2,1)} copy(bf16[64,256,32,32]{1,0,2,3:T(8,128)(2,1)} %convert_bitcast_fusion) | data formatting | bytes 67108864 | tf_op jit(solution)/shard_map/convert_element_type | solution.py:65
  1410.5 14.6 convert_reduce_fusion.2
  1426.9 16.4 fusion.210
  1443.3 17.3 fusion.116
  1467.0 105.2 %all-gather.21.cloned.1.call-done = bf16[256,256,128]{2,1,0:T(8,128)(2,1)} async-done(((bf16[64,256,128]{2,1,0:T(8,128)(2,1)}), bf16[256,256,128]{2,1,0:T(8,128)(2,1)}) %all-gather.21.cloned.1.call-update) | async-done | bytes 16777232 | tf_op jit(solution)/shard_map/all_gather | solution.py:96
  1572.2 21.8 copy.680
  1626.1 16.5 fusion.212
  1642.6 16.9 fusion.102
  1672.4 97.2 %all_to_all.118 = bf16[64,256,128]{2,0,1:T(8,128)(2,1)S(1)} all-to-all(bf16[64,256,128]{2,0,1:T(8,128)(2,1)} %copy.691), channel_id=1, replica_groups=mesh['req'=4,'dap'=4] {'dap'}, dimensions={1} | all-to-all | bytes 8388608 | tf_op jit(solution)/shard_map/all_to_all | solution.py:100
  1781.7 34.5 %all-gather.23.cloned.1.call-done = bf16[256,256,128]{2,1,0:T(8,128)(2,1)} async-done(((bf16[64,256,128]{2,1,0:T(8,128)(2,1)}), bf16[256,256,128]{2,1,0:T(8,128)(2,1)}) %all-gather.23.cloned.1.call-update) | async-done | bytes 16777232 | tf_op jit(solution)/shard_map/all_gather | solution.py:101
  1816.1 21.8 copy.694
  1889.2 31.9 %fusion.460 = (f32[64,4,256]{2,1,0:T(4,128)S(1)}, f32[64,4,256,256]{2,3,1,0:T(8,128)}) fusion(f32[4,256,256]{1,2,0:T(8,128)S(1)} %copy.702, pred[64,256]{1,0:T(8,128)(4,1)S(1)} %copy-done.56, bf16[64,256,4,32]{1,3,2,0:T(8,128)(2,1)} %bitcast.558, bf16[64,256,4,32]{1,3,2,0:T(8,128)(2,1)} %bitcast.557), kind=kOutput, calls=%fused_computation.622 | convolution fusion | flops 1157628160 | bytes 76824576 | tf_op jit(solution)/shard_map/sub | solution.py:37
  1921.0 26.4 %fusion.30 = f32[64,4,32,256]{3,2,1,0:T(8,128)} fusion(bf16[64,256,4,32]{1,3,2,0:T(8,128)(2,1)} %bitcast.555, f32[64,4,256,256]{2,3,1,0:T(8,128)} %get-tuple-element.81, f32[64,4,256]{2,1,0:T(4,128)S(1)} %get-tuple-element.80), kind=kOutput, calls=%fused_computation.52 | convolution fusion | flops 1107296256 | bytes 79953920 | tf_op jit(solution)/shard_map/bhqk,bkhd->bqhd/dot_general | solution.py:38
  1971.4 45.4 %all-to-all-done.8 = bf16[64,256,128]{2,0,1:T(8,128)(2,1)} async-done(((bf16[64,256,128]{2,0,1:T(8,128)(2,1)}), bf16[64,256,128]{2,0,1:T(8,128)(2,1)}, u32[]{:S(2)}, u32[]{:S(2)}) %all-to-all-start.8) | async-done | bytes 4194336 | tf_op jit(solution)/shard_map/all_to_all | solution.py:105
  2072.3 31.9 %fusion.461 = (f32[64,4,256]{2,1,0:T(4,128)S(1)}, f32[64,4,256,256]{2,3,1,0:T(8,128)}) fusion(f32[4,256,256]{1,2,0:T(8,128)S(1)} %copy.711, pred[64,256]{1,0:T(8,128)(4,1)S(1)} %copy-done.58, bf16[64,256,4,32]{1,3,2,0:T(8,128)(2,1)} %bitcast.554, bf16[64,256,4,32]{1,3,2,0:T(8,128)(2,1)} %bitcast.553), kind=kOutput, calls=%fused_computation.623 | convolution fusion | flops 1157628160 | bytes 76824576 | tf_op jit(solution)/shard_map/sub | solution.py:37
  2104.2 26.4 %fusion.31 = f32[64,4,32,256]{3,2,1,0:T(8,128)} fusion(bf16[64,256,4,32]{1,3,2,0:T(8,128)(2,1)} %bitcast.550, f32[64,4,256,256]{2,3,1,0:T(8,128)} %get-tuple-element.83, f32[64,4,256]{2,1,0:T(4,128)S(1)} %get-tuple-element.82), kind=kOutput, calls=%fused_computation.53 | convolution fusion | flops 1107296256 | bytes 79953920 | tf_op jit(solution)/shard_map/bhqk,bkhd->bqhd/dot_general | solution.py:38
  2154.1 44.7 %all-to-all-done.9 = bf16[256,64,128]{2,1,0:T(8,128)(2,1)} async-done(((bf16[256,64,128]{2,1,0:T(8,128)(2,1)}), bf16[256,64,128]{2,1,0:T(8,128)(2,1)}, u32[]{:S(2)}, u32[]{:S(2)}) %all-to-all-start.9) | async-done | bytes 4194336 | tf_op jit(solution)/shard_map/all_to_all | solution.py:108
  2226.9 13.2 fusion.162
  (446 shorter events, 794.8 us)
Async XLA Ops:
  7.2 41.7 %all-gather.9.cloned.1.call-start = ((), (), s32[]{:S(2)}) async-start(), calls=%async_computation.10 | async-start | bytes 1310720 | tf_op jit(solution)/shard_map/all_gather | solution.py:122
  34.1 7.8 copy-start.54
  48.8 21.6 copy-start.61
  98.7 29.3 %all-to-all-start = ((bf16[16,256,256]{2,0,1:T(8,128)(2,1)}), bf16[16,256,256]{2,0,1:T(8,128)(2,1)S(1)}, u32[]{:S(2)}, u32[]{:S(2)}) async-start(bf16[16,256,256]{2,0,1:T(8,128)(2,1)} %copy.570), calls=%async_computation | async-start | bytes 4194304 | tf_op jit(solution)/shard_map/all_to_all | solution.py:124
  102.3 144.3 %all-gather.11.cloned.1.call-start = ((), (), s32[]{:S(2)}) async-start(), calls=%async_computation.11 | async-start | bytes 2621440 | tf_op jit(solution)/shard_map/all_gather | solution.py:64
  102.5 60.5 %copy-start.59 = (pred[64,64]{1,0:T(8,128)(4,1)}, pred[64,64]{1,0:T(8,128)(4,1)S(1)}, u32[]{:S(2)}) copy-start(pred[64,64]{1,0:T(8,128)(4,1)S(1)} %copy.579) | copy-start | bytes 12292
  102.6 121.0 %copy-start.45 = (bf16[64,64]{1,0:T(8,128)(2,1)}, bf16[64,64]{1,0:T(8,128)(2,1)S(1)}, u32[]{:S(2)}) copy-start(bf16[64,64]{1,0:T(8,128)(2,1)S(1)} %dynamic-slice_convert_fusion.1) | copy-start | bytes 24580
  189.7 6.8 copy-start.73
  225.6 229.7 %all-gather.13.cloned.1.call-start = ((), (), s32[]{:S(2)}) async-start(), calls=%async_computation.12 | async-start | bytes 20971520 | tf_op jit(solution)/shard_map/all_gather | solution.py:96
  231.4 30.9 %copy-start.31 = (s32[256,256]{1,0:T(8,128)}, s32[256,256]{1,0:T(8,128)S(1)}, u32[]{:S(2)}) copy-start(s32[256,256]{1,0:T(8,128)S(1)} %all_gather.45) | copy-start | bytes 786436
  231.4 294.2 %copy-start.29 = (f32[64,256]{1,0:T(8,128)}, f32[64,256]{1,0:T(8,128)S(1)}, u32[]{:S(2)}) copy-start(f32[64,256]{1,0:T(8,128)S(1)} %dynamic-slice_convert_fusion) | copy-start | bytes 196612
  231.7 61.9 %copy-start.52 = (f32[64,256]{1,0:T(8,128)}, f32[64,256]{1,0:T(8,128)S(1)}, u32[]{:S(2)}) copy-start(f32[64,256]{1,0:T(8,128)S(1)} %convolution_add_fusion) | copy-start | bytes 196612
  262.3 31.3 %copy-start.69 = (bf16[2,1024,128]{2,1,0:T(8,128)(2,1)S(1)}, bf16[2,1024,128]{2,1,0:T(8,128)(2,1)}, u32[]{:S(2)}) copy-start(bf16[2,1024,128]{2,1,0:T(8,128)(2,1)} %param.37) | copy-start | bytes 1572868
  308.2 18.1 copy-start.16
  350.0 349.1 %all-gather.15.cloned.1.call-start = ((), (), s32[]{:S(2)}) async-start(), calls=%async_computation.13 | async-start | bytes 20971520 | tf_op jit(solution)/shard_map/all_gather | solution.py:101
  507.3 18.3 copy-start.10
  555.4 98.1 %all-to-all-start.2 = ((bf16[64,256,128]{2,0,1:T(8,128)(2,1)}), bf16[64,256,128]{2,0,1:T(8,128)(2,1)}, u32[]{:S(2)}, u32[]{:S(2)}) async-start(bf16[64,256,128]{2,0,1:T(8,128)(2,1)} %copy.616), calls=%async_computation.2 | async-start | bytes 8388608 | tf_op jit(solution)/shard_map/all_to_all | solution.py:100
  561.2 210.7 %copy-start.55 = (pred[64,256]{1,0:T(8,128)(4,1)}, pred[64,256]{1,0:T(8,128)(4,1)S(1)}, u32[]{:S(2)}) copy-start(pred[64,256]{1,0:T(8,128)(4,1)S(1)} %dynamic-slice_compare_fusion.1) | copy-start | bytes 49156
  743.5 8.7 copy-start.43
  830.1 6.0 copy-start.9
  830.1 6.0 copy-start.47
  846.5 52.9 %all-to-all-start.3 = ((bf16[64,256,128]{2,0,1:T(8,128)(2,1)}), bf16[64,256,128]{2,0,1:T(8,128)(2,1)}, u32[]{:S(2)}, u32[]{:S(2)}) async-start(bf16[64,256,128]{2,0,1:T(8,128)(2,1)} %copy.631), calls=%async_computation.3 | async-start | bytes 8388608 | tf_op jit(solution)/shard_map/all_to_all | solution.py:105
  851.8 103.1 %copy-start.57 = (pred[64,256]{1,0:T(8,128)(4,1)}, pred[64,256]{1,0:T(8,128)(4,1)S(1)}, u32[]{:S(2)}) copy-start(pred[64,256]{1,0:T(8,128)(4,1)S(1)} %copy.635) | copy-start | bytes 49156
  899.4 129.0 %all-to-all-start.1 = ((bf16[64,64,256]{2,1,0:T(8,128)(2,1)}), bf16[64,64,256]{2,1,0:T(8,128)(2,1)}, u32[]{:S(2)}, u32[]{:S(2)}) async-start(bf16[64,64,256]{2,1,0:T(8,128)(2,1)} %copy.586), calls=%async_computation.1 | async-start | bytes 4194304 | tf_op jit(solution)/shard_map/all_to_all | solution.py:131
  914.9 7.6 copy-start.1
  936.5 9.0 copy-start.63
  1028.4 52.7 %all-to-all-start.4 = ((bf16[256,64,128]{2,1,0:T(8,128)(2,1)}), bf16[256,64,128]{2,1,0:T(8,128)(2,1)}, u32[]{:S(2)}, u32[]{:S(2)}) async-start(bf16[256,64,128]{2,1,0:T(8,128)(2,1)} %copy.640), calls=%async_computation.4 | async-start | bytes 8388608 | tf_op jit(solution)/shard_map/all_to_all | solution.py:108
  1033.2 132.2 %all-gather.17.cloned.1.call-start = ((), (), s32[]{:S(2)}) async-start(), calls=%async_computation.14 | async-start | bytes 1310720 | tf_op jit(solution)/shard_map/all_gather | solution.py:122
  1109.3 9.1 copy-start.75
  1109.3 9.1 copy-start.77
  1138.3 225.2 %all-gather.19.cloned.1.call-start = ((), (), s32[]{:S(2)}) async-start(), calls=%async_computation.15 | async-start | bytes 2621440 | tf_op jit(solution)/shard_map/all_gather | solution.py:64
  1161.3 6.0 copy-start.62
  1306.7 6.8 copy-start.74
  1343.0 229.3 %all-gather.21.cloned.1.call-start = ((), (), s32[]{:S(2)}) async-start(), calls=%async_computation.16 | async-start | bytes 20971520 | tf_op jit(solution)/shard_map/all_gather | solution.py:96
  1379.1 31.4 %copy-start.53 = (f32[64,256]{1,0:T(8,128)S(1)}, f32[64,256]{1,0:T(8,128)}, u32[]{:S(2)}) copy-start(f32[64,256]{1,0:T(8,128)} %copy-done.52) | copy-start | bytes 196612
  1379.1 31.4 %copy-start.70 = (bf16[2,1024,128]{2,1,0:T(8,128)(2,1)S(1)}, bf16[2,1024,128]{2,1,0:T(8,128)(2,1)}, u32[]{:S(2)}) copy-start(bf16[2,1024,128]{2,1,0:T(8,128)(2,1)} %param.37) | copy-start | bytes 1572868
  1425.1 18.1 copy-start.14
  1426.9 16.4 copy-start.30
  1467.0 349.1 %all-gather.23.cloned.1.call-start = ((), (), s32[]{:S(2)}) async-start(), calls=%async_computation.17 | async-start | bytes 20971520 | tf_op jit(solution)/shard_map/all_gather | solution.py:101
  1624.3 18.3 copy-start.12
  1880.3 8.9 copy-start.56
  1947.4 6.0 copy-start.48
  1963.8 52.9 %all-to-all-start.8 = ((bf16[64,256,128]{2,0,1:T(8,128)(2,1)}), bf16[64,256,128]{2,0,1:T(8,128)(2,1)}, u32[]{:S(2)}, u32[]{:S(2)}) async-start(bf16[64,256,128]{2,0,1:T(8,128)(2,1)} %copy.706), calls=%async_computation.8 | async-start | bytes 8388608 | tf_op jit(solution)/shard_map/all_to_all | solution.py:105
  2016.7 129.1 %all-to-all-start.6 = ((bf16[64,64,256]{2,1,0:T(8,128)(2,1)}), bf16[64,64,256]{2,1,0:T(8,128)(2,1)}, u32[]{:S(2)}, u32[]{:S(2)}) async-start(bf16[64,64,256]{2,1,0:T(8,128)(2,1)} %copy.664), calls=%async_computation.6 | async-start | bytes 4194304 | tf_op jit(solution)/shard_map/all_to_all | solution.py:131
  2032.2 7.6 copy-start
  2045.7 8.2 copy-start.64
  2064.1 8.2 copy-start.58
  2145.9 52.9 %all-to-all-start.9 = ((bf16[256,64,128]{2,1,0:T(8,128)(2,1)}), bf16[256,64,128]{2,1,0:T(8,128)(2,1)}, u32[]{:S(2)}, u32[]{:S(2)}) async-start(bf16[256,64,128]{2,1,0:T(8,128)(2,1)} %copy.714), calls=%async_computation.9 | async-start | bytes 8388608 | tf_op jit(solution)/shard_map/all_to_all | solution.py:108
  (57 other events, 212.4 us)
Sparse Core Ops, SparseCore 0:
  20.6 17.4 all-gather.8
  225.7 20.9 all-gather.10
  350.1 105.0 all-gather.12
  549.1 150.0 all-gather.14
  1138.5 14.6 all-gather.16
  1343.1 20.4 all-gather.18
  1467.1 105.0 all-gather.20
  1666.1 150.0 all-gather.22
where the time goes:
time: 2260 us; the launch traced here: 2250 us
  matrix products  713 us (32%)
  waiting for transfers between devices  607 us (27%)
  local copies, waits for them, and re-layouts  456 us (20%)
  other arithmetic  249 us (11%)
  blocking collectives  168 us (7%)
  starting transfers between devices  37.9 us (2%)
    all_gather x4, waiting for transfers between devices, pair_stack(): right_full = lax.all_gather(right_act, GROUP_AXIS, axis=0, tiled=True)  276 us
    dot_general x34, matrix products, dense(): jnp.einsum('...c,cf->...f', x, weight, preferred_element_type=jnp.float32)  270 us
    sub x8, matrix products, attend(): attn_prob = jax.nn.softmax(logits, axis=-1).astype(jnp.bfloat16)  195 us
    dot_general x8, matrix products, attend(): jnp.einsum('bhqk,bkhd->bqhd', attn_prob, v_heads, preferred_element_type=...  163 us
    all_to_all x1, blocking collectives, pair_stack(): left_cols = lax.all_to_all(left_act, GROUP_AXIS, 1, 0, tiled=True)  97.2 us
    all_to_all x1, waiting for transfers between devices, pair_stack(): left_cols = lax.all_to_all(left_act, GROUP_AXIS, 1, 0, tiled=True)  92.3 us
    all_to_all x2, waiting for transfers between devices, pair_stack(): pair_cols = lax.all_to_all(pair_loc, GROUP_AXIS, 1, 0, tiled=True)  90.5 us
    all_to_all x2, waiting for transfers between devices, pair_stack(): lax.all_to_all(jnp.swapaxes(pair_t, 0, 1), GROUP_AXIS, 0, 1, tiled=True)  87.7 us
  transfers between devices with their start and end apart: 16, of which 12 were waited for; matrix products, arithmetic and copies ran while one was open for 15% of the time, Pallas kernels for 0%

commit v1 on v0

v1 whole, which is shorter than its diff:
```python
import functools

import jax
import jax.numpy as jnp
from jax import lax
from jax.experimental import pallas as pl
from jax.experimental.pallas import tpu as pltpu
from jax.sharding import PartitionSpec as P

GROUP_AXIS = 'dap'
PARTS_AXIS = 'req'
LOG2E = 1.4426950408889634
MASKED = -1e9 * LOG2E
HEAD = 32
F32 = jnp.float32
BF16 = jnp.bfloat16
VMEM_LIMIT = 60 * 1024 * 1024
NT = (((1,), (1,)), ((), ()))
NN = (((1,), (0,)), ((), ()))
TN = (((0,), (0,)), ((), ()))


def dot(x, y, dims=NN):
    return lax.dot_general(x, y, dims, preferred_element_type=F32)


def layer_norm(x):
    centered = x - jnp.mean(x, axis=-1, keepdims=True)
    variance = jnp.mean(centered * centered, axis=-1, keepdims=True)
    return (centered * lax.rsqrt(variance + 1e-5)).astype(BF16)


def call(body, name, grid, in_specs, out_specs, out_shape, scratch, flops, scalars=None):
    n_scalar = 0 if scalars is None else 1
    spec = pltpu.PrefetchScalarGridSpec(num_scalar_prefetch=n_scalar, grid=grid, in_specs=in_specs, out_specs=out_specs, scratch_shapes=scratch)
    return pl.pallas_call(
        body, name=name, grid_spec=spec, out_shape=out_shape,
        compiler_params=pltpu.CompilerParams(vmem_limit_bytes=VMEM_LIMIT, dimension_semantics=('arbitrary',) * len(grid)),
        cost_estimate=pl.CostEstimate(flops=flops, bytes_accessed=16 << 20, transcendentals=0))


def head_masks(width):
    lanes = lax.broadcasted_iota(jnp.int32, (1, width), 1) // HEAD
    keep = [lanes == h for h in range(width // HEAD)]
    return keep, [k.astype(F32).astype(BF16) for k in keep]


def attend(q, k, v, bias, key_ok):
    keep, mult = head_masks(q.shape[1])
    out = jnp.zeros(q.shape, F32)
    for h in range(len(keep)):
        logits = dot(q * mult[h], k, NT) * (HEAD ** -0.5 * LOG2E)
        if bias is not None:
            logits = logits + bias(h)
        logits = jnp.where(key_ok, logits, MASKED)
        top = jnp.max(logits, axis=-1, keepdims=True)
        weights = jnp.exp2(logits - top)
        prob = (weights * (1.0 / jnp.sum(weights, axis=-1, keepdims=True))).astype(BF16)
        out = jnp.where(keep[h], dot(prob, v), out)
    return out


def gated_attention(x_norm, w_qkvg, w_out, bias, key_ok):
    width = w_out.shape[0]
    proj = dot(x_norm, w_qkvg).astype(BF16)
    parts = []
    for g in range(width // 128):
        q, k, v, gate = (proj[:, p * width + g * 128:p * width + (g + 1) * 128] for p in range(4))
        attended = attend(q, k, v, None if bias is None else functools.partial(bias, g), key_ok)
        parts.append((attended * jax.nn.sigmoid(gate.astype(F32))).astype(BF16))
    gated = parts[0] if len(parts) == 1 else jnp.concatenate(parts, axis=1)
    return dot(gated, w_out)


def put_row(scr, r, value, step):
    for p in range(scr.shape[0]):
        scr[p, pl.ds(r, value.shape[0], stride=step), :] = value[:, p * 128:(p + 1) * 128]


def flush_rows(scr, out_ref, step):
    n = scr.shape[1] // step
    for p in range(scr.shape[0]):
        out_ref[:, :, p * 128:(p + 1) * 128] = scr[p].reshape(n, step, 128)[:out_ref.shape[0]].astype(BF16)


def whole(shape):
    return pl.BlockSpec(shape, lambda *_: (0,) * len(shape))


def layer_w(w, layer):
    return pl.BlockSpec((None,) + w.shape[1:], lambda *_: (layer, 0, 0))


def row_bias(z, w_t, layer):
    rows, cols, dim = z.shape
    heads = w_t.shape[1]
    step = 16

    def body(z_ref, w_ref, out_ref, scr):
        def one(r, carry):
            x = layer_norm(z_ref[r].astype(F32))
            put_row(scr, r, dot(w_ref[...], x, NT), step)
            return carry
        lax.fori_loop(0, step, one, 0)
        flush_rows(scr, out_ref, step)

    return call(body, 'row_bias', (rows // step,),
                [pl.BlockSpec((step, cols, dim), lambda i: (i, 0, 0)), layer_w(w_t, layer)],
                pl.BlockSpec((heads, step, cols), lambda i: (0, i, 0)),
                jax.ShapeDtypeStruct((heads, rows, cols), BF16),
                [pltpu.VMEM((cols // 128, heads * step, 128), F32)], 10 ** 9)(z, w_t)


def fill_bias(bias_ref, scr, swap):
    blocks, heads, rows, cols = bias_ref.shape
    for h in range(heads):
        full = jnp.concatenate([bias_ref[b, h].astype(F32) for b in range(blocks)], axis=0) * LOG2E
        scr[h] = full.T if swap else full


def row_attention(m, bias, mask, w_qkvg, w_out, layer, swap):
    n_seq, res, dim = m.shape
    heads = bias.shape[1]

    def body(m_ref, bias_ref, mask_ref, wq_ref, wo_ref, out_ref, scr):
        @pl.when(pl.program_id(0) == 0)
        def _():
            fill_bias(bias_ref, scr, swap)
        x = m_ref[0].astype(F32)
        update = gated_attention(layer_norm(x), wq_ref[...], wo_ref[...], lambda g, h: scr[g * 4 + h], mask_ref[0] > 0)
        out_ref[0] = (x + update).astype(BF16)

    return call(body, 'row_attention', (n_seq,),
                [pl.BlockSpec((1, res, dim), lambda s: (s, 0, 0)), whole(bias.shape),
                 pl.BlockSpec((1, 1, res), lambda s: (s, 0, 0)), layer_w(w_qkvg, layer), layer_w(w_out, layer)],
                pl.BlockSpec((1, res, dim), lambda s: (s, 0, 0)), jax.ShapeDtypeStruct(m.shape, BF16),
                [pltpu.VMEM((heads, res, res), F32)], 4 * 10 ** 10)(m, bias, mask, w_qkvg, w_out)


def column_stage(m, mask_t, w_qkvg, w_out, w_in, w_down, w_opm_t, layer):
    n_seq, res, dim = m.shape
    step = 16
    opm = w_opm_t.shape[1]

    def body(m_ref, mask_ref, wq_ref, wo_ref, wi_ref, wd_ref, wp_ref, out_ref, ab_ref, lo, hi, x_scr, att):
        halves = (lo, hi)
        for p in range(2):
            halves[p][...] = m_ref[:, :, p * 128:(p + 1) * 128].astype(F32).reshape(n_seq * step, 128)

        def gather(r, carry):
            at = pl.ds(pl.multiple_of(r * n_seq, n_seq), n_seq)
            for p in range(2):
                x_scr[at, p * 128:(p + 1) * 128] = halves[p][pl.ds(r, n_seq, stride=step), :]
            return carry
        lax.fori_loop(0, step, gather, 0)

        def one(r, carry):
            at = pl.ds(pl.multiple_of(r * n_seq, n_seq), n_seq)
            proj = dot(layer_norm(x_scr[at, :]), wq_ref[...]).astype(BF16)
            key_ok = mask_ref[r] > 0
            keep, mult = head_masks(128)
            for g in range(2):
                q, k, v, gate = (proj[:, p * 256 + g * 128:p * 256 + (g + 1) * 128] for p in range(4))
                stacked = jnp.concatenate([q * mult[h] for h in range(4)], axis=0)
                logits = dot(stacked, k, NT) * (HEAD ** -0.5 * LOG2E)
                logits = jnp.where(key_ok, logits, MASKED)
                weights = jnp.exp2(logits - jnp.max(logits, axis=-1, keepdims=True))
                prob = (weights * (1.0 / jnp.sum(weights, axis=-1, keepdims=True))).astype(BF16)
                full = dot(prob, v)
                attended = jnp.zeros((n_seq, 128), F32)
                for h in range(4):
                    attended = jnp.where(keep[h], full[h * n_seq:(h + 1) * n_seq], attended)
                att[at, g * 128:(g + 1) * 128] = (attended * jax.nn.sigmoid(gate.astype(F32))).astype(BF16)
            return carry
        lax.fori_loop(0, step, one, 0)

        x = x_scr[...] + dot(att[...], wo_ref[...])
        x = x.astype(BF16).astype(F32)
        hidden = jnp.maximum(dot(layer_norm(x), wi_ref[...]), 0.0).astype(BF16)
        x = (x + dot(hidden, wd_ref[...])).astype(BF16).astype(F32)
        x_scr[...] = x

        def project(r, carry):
            at = pl.ds(pl.multiple_of(r * n_seq, n_seq), n_seq)
            x_r = x_scr[at, :]
            ab = dot(wp_ref[...], layer_norm(x_r), NT).astype(BF16)
            ab_ref[r] = (ab.astype(F32) * mask_ref[r].astype(F32)).astype(BF16)
            for p in range(2):
                halves[p][pl.ds(r, n_seq, stride=step), :] = x_r[:, p * 128:(p + 1) * 128]
            return carry
        lax.fori_loop(0, step, project, 0)
        for p in range(2):
            out_ref[:, :, p * 128:(p + 1) * 128] = halves[p][...].reshape(n_seq, step, 128).astype(BF16)

    return call(body, 'column_stage', (res // step,),
                [pl.BlockSpec((n_seq, step, dim), lambda i: (0, i, 0)), pl.BlockSpec((step, 1, n_seq), lambda i: (i, 0, 0))]
                + [layer_w(w, layer) for w in (w_qkvg, w_out, w_in, w_down, w_opm_t)],
                (pl.BlockSpec((n_seq, step, dim), lambda i: (0, i, 0)), pl.BlockSpec((step, opm, n_seq), lambda i: (i, 0, 0))),
                (jax.ShapeDtypeStruct(m.shape, BF16), jax.ShapeDtypeStruct((res, opm, n_seq), BF16)),
                [pltpu.VMEM((n_seq * step, 128), F32), pltpu.VMEM((n_seq * step, 128), F32),
                 pltpu.VMEM((n_seq * step, dim), F32), pltpu.VMEM((n_seq * step, dim), BF16)],
                4 * 10 ** 10)(m, mask_t, w_qkvg, w_out, w_in, w_down, w_opm_t)


def outer_product(z, left, right, mask_left, mask_right, w_opm, where, layer, by_cols):
    opm = w_opm.shape[2] // 32
    res = right.shape[1]
    n_seq = right.shape[2]
    step = 8
    half = res // 2

    def body(where_ref, z_ref, left_ref, right_ref, ml_ref, mr_ref, w_ref, out_ref, pairs):
        lhs = left_ref[...].reshape(step * opm, n_seq)

        def outer(e, carry):
            full = dot(lhs, right_ref[e], NT).astype(BF16)
            at = pl.ds(pl.multiple_of(e * opm, opm), opm)
            for r in range(step):
                pairs[r, at, :] = full[r * opm:(r + 1) * opm]
            return carry
        lax.fori_loop(0, opm, outer, 0, unroll=4)
        overlap = dot(ml_ref[...], mr_ref[...])
        scale = 1.0 / (1e-3 + overlap)
        for r in range(step):
            update = dot(w_ref[...], pairs[r]) * scale[r:r + 1]
            if by_cols:
                old = jnp.concatenate([z_ref[b, r] for b in range(z_ref.shape[0])], axis=0)
            else:
                old = z_ref[0, r]
            out_ref[r] = (old.astype(F32) + update.T).astype(BF16)

    blocks = z.shape[0]
    per_block = res // blocks // step
    if by_cols:
        z_spec = pl.BlockSpec((blocks, step, z.shape[2], z.shape[3]), lambda t, s: (0, ((t // per_block) * 2 + s[0]) * per_block + t % per_block, 0, 0))
    else:
        z_spec = pl.BlockSpec((1, step, z.shape[2], z.shape[3]), lambda t, s: ((t // per_block) * 2 + s[0], t % per_block, 0, 0))
    row_of = lambda t, s: ((t // per_block) * 2 + s[0]) * per_block + t % per_block
    return call(body, 'outer_product', (half // step,),
                [z_spec, pl.BlockSpec((step, opm, n_seq), lambda t, s: (row_of(t, s), 0, 0)), whole(right.shape),
                 pl.BlockSpec((step, n_seq), lambda t, s: (row_of(t, s), 0)), whole(mask_right.shape), layer_w(w_opm, layer)],
                pl.BlockSpec((step, res, z.shape[3]), lambda t, s: (t, 0, 0)),
                jax.ShapeDtypeStruct((half, res, z.shape[3]), BF16),
                [pltpu.VMEM((step, opm * opm, res), BF16)], 2 * 10 ** 10, where)(where, z, left, right, mask_left, mask_right, w_opm)


def triangle_project(z, mask, w_t, where, layer, chip_cols):
    rows, cols, dim = z.shape
    tri = (w_t.shape[1] - dim) // 4
    step = 16
    a_cols = cols // 2 if chip_cols else cols

    def body(where_ref, z_ref, mask_ref, w_ref, a_ref, b_ref, a_scr, b_scr):
        def one(r, carry):
            x = layer_norm(z_ref[r].astype(F32))
            proj = dot(w_ref[:4 * tri, :], x, NT)
            mask_row = mask_ref[r]
            a, b, ga, gb = (proj[p * tri:(p + 1) * tri] for p in range(4))
            mask_a = mask_row
            if chip_cols:
                first = where_ref[1] == 0
                a, ga, mask_a = (jnp.where(first, v[:, :a_cols], v[:, a_cols:]) for v in (a, ga, mask_row))
            a = mask_a * jax.nn.sigmoid(ga) * a
            b = mask_row * jax.nn.sigmoid(gb) * b
            put_row(a_scr, r, a, step)
            put_row(b_scr, r, b, step)
            return carry
        lax.fori_loop(0, step, one, 0)
        flush_rows(a_scr, a_ref, step)
        flush_rows(b_scr, b_ref, step)

    return call(body, 'triangle_project', (rows // step,),
                [pl.BlockSpec((step, cols, dim), lambda i, s: (i, 0, 0)), pl.BlockSpec((step, 1, cols), lambda i, s: (i, 0, 0)), layer_w(w_t, layer)],
                (pl.BlockSpec((tri, step, a_cols), lambda i, s: (0, i, 0)), pl.BlockSpec((tri, step, cols), lambda i, s: (0, i, 0))),
                (jax.ShapeDtypeStruct((tri, rows, a_cols), BF16), jax.ShapeDtypeStruct((tri, rows, cols), BF16)),
                [pltpu.VMEM((a_cols // 128, tri * step, 128), F32), pltpu.VMEM((cols // 128, tri * step, 128), F32)],
                2 * 10 ** 10, where)(where, z, mask, w_t)


def triangle_finish(z, a, b, w_proj, w_out, where, layer, incoming, w_bias_t=None):
    half, res, dim = z.shape
    tri = b.shape[1]
    quarter = half // 2
    rows_out = quarter if incoming else half
    ch = 8
    step = 16
    n_prod = tri // ch
    n_fin = rows_out // step
    heads = 0 if w_bias_t is None else w_bias_t.shape[1]
    pad = 8

    def body(where_ref, z_ref, a_ref, b_ref, wp_ref, wo_ref, *rest):
        if heads:
            wb_ref, out_ref, bias_ref, prod, norm, bias_scr = rest
        else:
            out_ref, prod, norm = rest
        t = pl.program_id(0)

        @pl.when(t < n_prod)
        def _():
            for c in range(ch):
                if incoming:
                    x = dot(a_ref[0, c], b_ref[0, c], TN) + dot(a_ref[1, c], b_ref[1, c], TN)
                else:
                    rhs = jnp.concatenate([b_ref[0, c, :quarter], b_ref[1, c, :quarter], b_ref[0, c, quarter:], b_ref[1, c, quarter:]], axis=0)
                    x = dot(a_ref[c], rhs, NT)
                prod[t * ch + c] = x

        @pl.when(t >= n_prod)
        def _():
            first = (t - n_prod) * step
            if incoming:
                first = first + where_ref[0] * quarter
            x = prod[:, pl.ds(pl.multiple_of(first, step), step), :]
            centered = x - jnp.mean(x, axis=0, keepdims=True)
            variance = jnp.mean(centered * centered, axis=0, keepdims=True)
            normed = centered * lax.rsqrt(variance + 1e-5)
            for p in range(res // 128):
                norm[p] = normed[:, :, p * 128:(p + 1) * 128].reshape(tri * step, 128)

            def one(r, carry):
                z_r = z_ref[r].astype(F32)
                gate = jax.nn.sigmoid(dot(layer_norm(z_r), wp_ref[:, 4 * tri:]))
                update = jnp.concatenate([dot(norm[p, pl.ds(r, tri, stride=step), :].astype(BF16), wo_ref[...], TN) for p in range(res // 128)], axis=0)
                new = (z_r + gate * update).astype(BF16)
                out_ref[r] = new
                if heads:
                    put_row(bias_scr, r, dot(wb_ref[...], layer_norm(new.astype(F32)), NT), step)
                return carry
            lax.fori_loop(0, step, one, 0)
            if heads:
                flush_rows(bias_scr, bias_ref, step)

    fin = lambda t: jnp.maximum(t - n_prod, 0)
    first_row = (lambda s: s[1] * (quarter // step)) if incoming else (lambda s: 0)
    prod_at = lambda t: jnp.minimum(t, n_prod - 1)
    if incoming:
        a_spec = pl.BlockSpec((2, ch) + a.shape[2:], lambda t, s: (0, prod_at(t), 0, 0))
    else:
        a_spec = pl.BlockSpec((ch,) + a.shape[1:], lambda t, s: (prod_at(t), 0, 0))
    n_heads = heads and 4
    in_specs = [pl.BlockSpec((step, res, dim), lambda t, s: (first_row(s) + fin(t), 0, 0)), a_spec,
                pl.BlockSpec((2, ch) + b.shape[2:], lambda t, s: (0, prod_at(t), 0, 0)), layer_w(w_proj, layer), layer_w(w_out, layer)]
    out_specs = [pl.BlockSpec((step, res, dim), lambda t, s: (fin(t), 0, 0))]
    out_shape = [jax.ShapeDtypeStruct((rows_out, res, dim), BF16)]
    rows_prod = a.shape[-1] if incoming else half
    scratch = [pltpu.VMEM((tri, rows_prod, res), F32), pltpu.VMEM((res // 128, tri * step, 128), F32)]
    args = [where, z, a, b, w_proj, w_out]
    if heads:
        in_specs.append(layer_w(w_bias_t, layer))
        out_specs.append(pl.BlockSpec((n_heads, step, res), lambda t, s: (0, fin(t), 0)))
        out_shape.append(jax.ShapeDtypeStruct((n_heads, rows_out, res), BF16))
        scratch.append(pltpu.VMEM((res // 128, pad * step, 128), F32))
        args.append(w_bias_t)
    return call(body, 'triangle_in' if incoming else 'triangle_out', (n_prod + n_fin,), in_specs, tuple(out_specs), tuple(out_shape), scratch, 2 * 10 ** 10, where)(*args)


def start_attention(z, bias, mask, w_qkvg, w_out, w_bias_t, layer):
    rows, res, dim = z.shape
    heads = bias.shape[1]
    step = 16
    pad = w_bias_t.shape[1]

    def body(z_ref, bias_ref, mask_ref, wq_ref, wo_ref, wb_ref, out_ref, next_ref, scr, bias_scr):
        @pl.when(pl.program_id(0) == 0)
        def _():
            fill_bias(bias_ref, scr, False)

        def one(r, carry):
            x = z_ref[r].astype(F32)
            update = gated_attention(layer_norm(x), wq_ref[...], wo_ref[...], lambda g, h: scr[h], mask_ref[r] > 0)
            new = (x + update).astype(BF16)
            out_ref[r] = new
            put_row(bias_scr, r, dot(wb_ref[...], layer_norm(new.astype(F32)), NT), step)
            return carry
        lax.fori_loop(0, step, one, 0)
        flush_rows(bias_scr, next_ref, step)

    return call(body, 'start_attention', (rows // step,),
                [pl.BlockSpec((step, res, dim), lambda i: (i, 0, 0)), whole(bias.shape), pl.BlockSpec((step, 1, res), lambda i: (i, 0, 0)),
                 layer_w(w_qkvg, layer), layer_w(w_out, layer), layer_w(w_bias_t, layer)],
                (pl.BlockSpec((step, res, dim), lambda i: (i, 0, 0)), pl.BlockSpec((heads, step, res), lambda i: (0, i, 0))),
                (jax.ShapeDtypeStruct(z.shape, BF16), jax.ShapeDtypeStruct((heads, rows, res), BF16)),
                [pltpu.VMEM((heads, res, res), F32), pltpu.VMEM((res // 128, pad * step, 128), F32)],
                5 * 10 ** 10)(z, bias, mask, w_qkvg, w_out, w_bias_t)


def end_stage(z, bias, mask_t, w_qkvg, w_out, w_in, w_down, w_bias_t, layer, next_layer):
    res, cols, dim = z.shape
    heads = bias.shape[1]
    step = 16
    pad = w_bias_t.shape[1]

    def body(z_ref, bias_ref, mask_ref, wq_ref, wo_ref, wi_ref, wd_ref, wb_ref, out_ref, next_ref, scr, rows, bias_scr):
        @pl.when(pl.program_id(0) == 0)
        def _():
            fill_bias(bias_ref, scr, True)
        rows[...] = z_ref[...].astype(F32).reshape(res * step, dim)

        def one(r, carry):
            at = pl.ds(r, res, stride=step)
            x = rows[at, :]
            x = x + gated_attention(layer_norm(x), wq_ref[...], wo_ref[...], lambda g, h: scr[h], mask_ref[r] > 0)
            x = x.astype(BF16).astype(F32)
            hidden = jnp.maximum(dot(layer_norm(x), wi_ref[...]), 0.0).astype(BF16)
            x = (x + dot(hidden, wd_ref[...])).astype(BF16).astype(F32)
            rows[at, :] = x
            put_row(bias_scr, r, dot(wb_ref[...], layer_norm(x), NT), step)
            return carry
        lax.fori_loop(0, step, one, 0)
        out_ref[...] = rows[...].reshape(res, step, dim).astype(BF16)
        flush_rows(bias_scr, next_ref, step)

    return call(body, 'end_stage', (cols // step,),
                [pl.BlockSpec((res, step, dim), lambda i: (0, i, 0)), whole(bias.shape), pl.BlockSpec((step, 1, res), lambda i: (i, 0, 0))]
                + [layer_w(w, layer) for w in (w_qkvg, w_out, w_in, w_down)] + [layer_w(w_bias_t, next_layer)],
                (pl.BlockSpec((res, step, dim), lambda i: (0, i, 0)), pl.BlockSpec((pad, step, res), lambda i: (0, i, 0))),
                (jax.ShapeDtypeStruct(z.shape, BF16), jax.ShapeDtypeStruct((pad, cols, res), BF16)),
                [pltpu.VMEM((heads, res, res), F32), pltpu.VMEM((res * step, dim), F32), pltpu.VMEM((res // 128, pad * step, 128), F32)],
                6 * 10 ** 10)(z, bias, mask_t, w_qkvg, w_out, w_in, w_down, w_bias_t)


def gather(x):
    return lax.all_gather(x, GROUP_AXIS, axis=0)


def pair_gather(x):
    return lax.all_gather(x, GROUP_AXIS, axis=0, axis_index_groups=[[0, 1], [2, 3]])


def transpose_w(w, pad=0):
    w = jnp.swapaxes(w, 1, 2)
    return jnp.pad(w, ((0, 0), (0, pad), (0, 0))) if pad else w


def solution(mesh):
    row_spec = P((PARTS_AXIS, GROUP_AXIS))

    def local_body(m, z, msa_mask, pair_mask, *weights):
        (row_qkvg, row_bias_w, row_out, col_qkvg, col_out, mtr_in, mtr_out, opm_proj, opm_out,
         tmo_proj, tmo_out, tmi_proj, tmi_out, tas_qkvg, tas_bias, tas_out,
         tae_qkvg, tae_bias, tae_out, ptr_in, ptr_out) = weights
        layers = row_qkvg.shape[0]
        shard = lax.axis_index(GROUP_AXIS)
        chip, core = shard // 2, shard % 2
        where = jnp.stack([core, chip]).astype(jnp.int32)
        n_seq, res_loc = m.shape[0], z.shape[0]
        res = z.shape[1]
        z_all = gather(z)
        full_mask = lax.all_gather(msa_mask, GROUP_AXIS, axis=0, tiled=True)
        full_pair = lax.all_gather(pair_mask, GROUP_AXIS, axis=0)
        seq_mask = msa_mask[:, None, :]
        res_mask_t = lax.dynamic_slice_in_dim(full_mask, shard * res_loc, res_loc, 1).T[:, None, :]
        mask_bf = full_mask.astype(BF16)
        mask_bf_t = mask_bf.T
        half_mask = lax.dynamic_index_in_dim(full_pair.reshape(2, 2, res_loc, res), core, 1, False)
        half_mask = half_mask.reshape(2 * res_loc, 1, res).astype(F32)
        row_mask = pair_mask[:, None, :]
        col_mask = lax.dynamic_slice_in_dim(full_pair.reshape(res, res), shard * res_loc, res_loc, 1).T[:, None, :]
        row_bias_t = transpose_w(row_bias_w)
        tas_bias_t, tae_bias_t = transpose_w(tas_bias, 4), transpose_w(tae_bias, 4)
        tmo_t, tmi_t, opm_proj_t = transpose_w(tmo_proj), transpose_w(tmi_proj), transpose_w(opm_proj)
        opm = opm_proj.shape[2] // 2
        opm_t = opm_out.reshape(layers, opm, opm, -1).transpose(0, 3, 2, 1).reshape(layers, -1, opm * opm)

        bias = row_bias(z, row_bias_t, 0)
        for layer in range(layers):
            by_cols = layer > 0
            if by_cols:
                z_all = gather(z)
            m = row_attention(m, gather(bias), seq_mask, row_qkvg, row_out, layer, by_cols)
            m = lax.all_to_all(m, GROUP_AXIS, 1, 0, tiled=True)
            m, ab = column_stage(m, res_mask_t, col_qkvg, col_out, mtr_in, mtr_out, opm_proj_t, layer)
            ab = gather(ab).reshape(res, 2 * opm, -1)
            right = jnp.swapaxes(ab[:, opm:], 0, 1)
            m = lax.all_to_all(m, GROUP_AXIS, 0, 1, tiled=True)
            half = outer_product(z_all, ab, right, mask_bf_t, mask_bf, opm_t, where, layer, by_cols)
            a, b = triangle_project(half, half_mask, tmo_t, where, layer, False)
            half, = triangle_finish(half, a, pair_gather(b), tmo_proj, tmo_out, where, layer, False)
            a, b = triangle_project(half, half_mask, tmi_t, where, layer, True)
            z, bias = triangle_finish(half, pair_gather(a), pair_gather(b), tmi_proj, tmi_out, where, layer, True, tas_bias_t)
            z, bias = start_attention(z, gather(bias), row_mask, tas_qkvg, tas_out, tae_bias_t, layer)
            bias = gather(bias)
            z = lax.all_to_all(z, GROUP_AXIS, 1, 0, tiled=True)
            z, bias = end_stage(z, bias, col_mask, tae_qkvg, tae_out, ptr_in, ptr_out, row_bias_t, layer, min(layer + 1, layers - 1))
        return m, lax.all_to_all(z, GROUP_AXIS, 0, 1, tiled=True)

    def run_blocks(*arrays):
        n_weights = len(arrays) - 4
        return jax.shard_map(local_body, mesh=mesh, in_specs=(row_spec,) * 4 + (P(),) * n_weights, out_specs=(row_spec, row_spec), check_vma=False)(*arrays)

    return run_blocks
```

time: 2260 us -> 2200 us (0.973)
  Pallas kernels: 0 us -> 1400 us
  matrix products: 713 us -> 0 us
  local copies, waits for them, and re-layouts: 456 us -> 80.2 us
  other arithmetic: 249 us -> 1.25 us
  waiting for transfers between devices: 607 us -> 484 us
    pallas_call x0 -> x19, Pallas kernels: none -> 1400 us  [the longest x2 279 us: end_stage(): call(body, 'end_stage', (cols // step,), [pl.BlockSpec((res, step, dim),...]
    dot_general x55 -> x0, matrix products: 518 us -> none  [the longest x34 270 us: dense(): jnp.einsum('...c,cf->...f', x, weight, preferred_element_type=jnp.float32)]
    all_to_all x8 -> x6, waiting for transfers between devices: 296 us -> 46.5 us  [the longest x1 46.4 us: local_body(): return (m, lax.all_to_all(z, GROUP_AXIS, 0, 1, tiled=True))]
    sub x8 -> x0, matrix products: 195 us -> none  [attend(): attn_prob = jax.nn.softmax(logits, axis=-1).astype(jnp.bfloat16)]
    convert_element_type x32 -> x1, local copies, waits for them, and re-layouts: 183 us -> 0.79 us  [local_body(): half_mask = half_mask.reshape(2 * res_loc, 1, res).astype(F32)]
    convert_element_type x36 -> x2, other arithmetic: 158 us -> 0.63 us  [the longest x1 0.62 us: local_body(): mask_bf = full_mask.astype(BF16)]
    all_gather x8 -> x12, waiting for transfers between devices: 311 us -> 435 us  [the longest x6 279 us: gather(): return lax.all_gather(x, GROUP_AXIS, axis=0)]
    all_gather x6, blocking collectives: 42.5 us -> 153 us  [the longest x4 120 us: gather(): return lax.all_gather(x, GROUP_AXIS, axis=0)]
  transfers between devices with their start and end apart: 16 -> 18, of which waited for: 12 -> 13; matrix products, arithmetic and copies ran while one was open for 15% -> 2% of each run, Pallas kernels for 0% -> 13%
where the time goes in v1:
time: 2200 us; the launch traced here: 2190 us
  Pallas kernels  1400 us (64%)
  waiting for transfers between devices  484 us (22%)
  blocking collectives  181 us (8%)
  local copies, waits for them, and re-layouts  80.2 us (4%)
  starting transfers between devices  26.9 us (1%)
    pallas_call x2, Pallas kernels, end_stage(): call(body, 'end_stage', (cols // step,), [pl.BlockSpec((res, step, dim),...  279 us
    all_gather x6, waiting for transfers between devices, gather(): return lax.all_gather(x, GROUP_AXIS, axis=0)  279 us
    pallas_call x4, Pallas kernels, triangle_finish(): call(body, 'triangle_in' if incoming else 'triangle_out', (n_prod + n_fin...  265 us
    pallas_call x4, Pallas kernels, triangle_project(): call(body, 'triangle_project', (rows // step,), [pl.BlockSpec((step, cols...  257 us
    pallas_call x2, Pallas kernels, start_attention(): call(body, 'start_attention', (rows // step,), [pl.BlockSpec((step, res,...  222 us
    pallas_call x2, Pallas kernels, column_stage(): call(body, 'column_stage', (res // step,), [pl.BlockSpec((n_seq, step, di...  172 us
    all_gather x6, waiting for transfers between devices, pair_gather(): lax.all_gather(x, GROUP_AXIS, axis=0, axis_index_groups=[[0, 1], [2, 3]])  156 us
    all_gather x4, blocking collectives, gather(): return lax.all_gather(x, GROUP_AXIS, axis=0)  120 us
  transfers between devices with their start and end apart: 18, of which 13 were waited for; matrix products, arithmetic and copies ran while one was open for 2% of the time, Pallas kernels for 13%

profile of v1, /device:TPU:0, one launch (start us, length us, event | category | flops | bytes accessed | tf_op | source)
XLA Modules:
  0.0 2188.9 jit_solution(14675805177436725622)
XLA Ops:
  7.2 22.3 %row_bias.1 = bf16[8,64,256]{2,1,0:T(8,128)(2,1)} custom-call(bf16[64,256,128]{2,1,0:T(8,128)(2,1)} %z_ref.1, bf16[2,8,128]{2,1,0:T(8,128)(2,1)} %bitcast.91), custom_call_target="tpu_custom_call" | custom-call | flops 1000000000 | bytes 16777216 | tf_op jit(solution)/shard_map/row_bias/pallas_call | solution.py:107
  30.1 17.0 all-gather.30.cloned.1.call-done
  47.1 34.3 %row_attention.2 = bf16[16,256,256]{2,1,0:T(8,128)(2,1)} custom-call(bf16[16,256,256]{2,1,0:T(8,128)(2,1)} %m_ref.1, bf16[4,8,64,256]{3,2,1,0:T(8,128)(2,1)} %bitcast.105, s32[16,1,256]{2,1,0:T(1,128)} %broadcast_in_dim.12.mask_ref, bf16[2,256,1024]{2,1,0:T(8,128)(2,1)} %wq_ref.12, bf16[2,256,256]{2,1,0:T(8,128)(2,1)} %wo_ref.18), custom_call_target="tpu_custom_call" | custom-call | flops 40000000000 | bytes 16777216 | tf_op jit(solution)/shard_map/row_attention/pallas_call | solution.py:133
  89.2 26.5 %all_gather.107 = s32[64,256]{1,0:T(8,128)S(1)} all-gather(s32[16,256]{1,0:T(8,128)S(1)} %copy-done.10), channel_id=1, replica_groups=mesh['req'=4,'dap'=4] {'dap'}, dimensions={0}, use_global_device_ids=true | all-gather | bytes 81920 | tf_op jit(solution)/shard_map/all_gather | solution.py:450
  118.6 86.0 %column_stage.2 = (bf16[64,64,256]{2,1,0:T(8,128)(2,1)}, bf16[64,64,64]{2,1,0:T(8,128)(2,1)}) custom-call(bf16[64,64,256]{2,1,0:T(8,128)(2,1)} %bitcast.78, s32[64,1,64]{2,1,0:T(1,128)} %copy.92.mask_ref, bf16[2,256,1024]{2,1,0:T(8,128)(2,1)} %wq_ref.13, bf16[2,256,256]{2,1,0:T(8,128)(2,1)} %wo_ref.19, bf16[2,256,1024]{2,1,0:T(8,128)(2,1)} %wi_ref.6, ...), custom_call_target="tpu_custom_call" | custom-call | flops 40000000000 | bytes 16777216 | tf_op jit(solution)/shard_map/column_stage/pallas_call | solution.py:195
  209.7 6.3 all-gather.3
  220.2 19.9 all-gather.34.cloned.1.call-done
  240.1 7.0 copy.96.left_ref
  248.7 98.1 %all-gather.32.cloned.1.call-done = bf16[256,256,128]{2,1,0:T(8,128)(2,1)} async-done(((bf16[64,256,128]{2,1,0:T(8,128)(2,1)}), bf16[256,256,128]{2,1,0:T(8,128)(2,1)}) %all-gather.32.cloned.1.call-update) | async-done | bytes 16777232 | tf_op jit(solution)/shard_map/all_gather | solution.py:424
  346.8 57.3 %outer_product.2.z_ref = bf16[128,256,128]{2,1,0:T(8,128)(2,1)} custom-call(s32[2]{0:T(128)} %pad_add_fusion.where_ref, bf16[4,64,256,128]{3,2,1,0:T(8,128)(2,1)} %bitcast.96, bf16[256,64,64]{2,1,0:T(8,128)(2,1)} %copy.96.left_ref, bf16[32,256,64]{2,1,0:T(8,128)(2,1)} %slice_bitcast_fusion.1.right_ref, bf16[256,64]{1,0:T(8,128)(2,1)} %copy.97.ml_ref, ...), custom_call_target="tpu_custom_call" | custom-call | flops 20000000000 | bytes 16777216 | tf_op jit(solution)/shard_map/outer_product/pallas_call | solution.py:239
  404.1 66.5 %triangle_project.4 = (bf16[128,128,256]{2,1,0:T(8,128)(2,1)}, bf16[128,128,256]{2,1,0:T(8,128)(2,1)}) custom-call(s32[2]{0:T(128)} %pad_add_fusion.where_ref, bf16[128,256,128]{2,1,0:T(8,128)(2,1)} %outer_product.2.z_ref, f32[128,1,256]{2,1,0:T(1,128)} %convert_element_type.13.mask_ref, bf16[2,640,128]{2,1,0:T(8,128)(2,1)} %bitcast.86), custom_call_target="tpu_custom_call" | custom-call | flops 20000000000 | bytes 16777216 | tf_op jit(solution)/shard_map/triangle_project/pallas_call | solution.py:272
  472.5 27.0 %all-gather.36.cloned.1.call-done = bf16[256,128,256]{2,1,0:T(8,128)(2,1)} async-done(((bf16[128,128,256]{2,1,0:T(8,128)(2,1)}), bf16[256,128,256]{2,1,0:T(8,128)(2,1)}) %all-gather.36.cloned.1.call-update) | async-done | bytes 16777232 | tf_op jit(solution)/shard_map/all_gather | solution.py:428
  499.5 69.6 %triangle_out.2.z_ref = bf16[128,256,128]{2,1,0:T(8,128)(2,1)} custom-call(s32[2]{0:T(128)} %pad_add_fusion.where_ref, bf16[128,256,128]{2,1,0:T(8,128)(2,1)} %outer_product.2.z_ref, bf16[128,128,256]{2,1,0:T(8,128)(2,1)} %get-tuple-element.27.a_ref, bf16[2,128,128,256]{3,2,1,0:T(8,128)(2,1)} %bitcast.100, bf16[2,128,640]{2,1,0:T(8,128)(2,1)} %wp_ref.6, ...), custom_call_target="tpu_custom_call" | custom-call | flops 20000000000 | bytes 16777216 | tf_op jit(solution)/shard_map/triangle_out/pallas_call | solution.py:355
  569.1 62.4 %triangle_project.5 = (bf16[128,128,128]{2,1,0:T(8,128)(2,1)}, bf16[128,128,256]{2,1,0:T(8,128)(2,1)}) custom-call(s32[2]{0:T(128)} %pad_add_fusion.where_ref, bf16[128,256,128]{2,1,0:T(8,128)(2,1)} %triangle_out.2.z_ref, f32[128,1,256]{2,1,0:T(1,128)} %convert_element_type.13.mask_ref, bf16[2,640,128]{2,1,0:T(8,128)(2,1)} %bitcast.88), custom_call_target="tpu_custom_call" | custom-call | flops 20000000000 | bytes 16777216 | tf_op jit(solution)/shard_map/triangle_project/pallas_call | solution.py:272
  634.0 17.8 all-gather.38.cloned.1.call-done
  651.8 31.3 %all-gather.40.cloned.1.call-done = bf16[256,128,256]{2,1,0:T(8,128)(2,1)} async-done(((bf16[128,128,256]{2,1,0:T(8,128)(2,1)}), bf16[256,128,256]{2,1,0:T(8,128)(2,1)}) %all-gather.40.cloned.1.call-update) | async-done | bytes 16777232 | tf_op jit(solution)/shard_map/all_gather | solution.py:428
  683.1 62.9 %triangle_in.2 = (bf16[64,256,128]{2,1,0:T(8,128)(2,1)}, bf16[4,64,256]{2,1,0:T(8,128)(2,1)}) custom-call(s32[2]{0:T(128)} %pad_add_fusion.where_ref, bf16[128,256,128]{2,1,0:T(8,128)(2,1)} %triangle_out.2.z_ref, bf16[2,128,128,128]{3,2,1,0:T(8,128)(2,1)} %bitcast.102, bf16[2,128,128,256]{3,2,1,0:T(8,128)(2,1)} %bitcast.97, bf16[2,128,640]{2,1,0:T(8,128)(2,1)} %wp_ref.7, ...), custom_call_target="tpu_custom_call" | custom-call | flops 20000000000 | bytes 16777216 | tf_op jit(solution)/shard_map/triangle_in/pallas_call | solution.py:355
  746.1 8.9 all-gather.7
  754.9 110.8 %start_attention.2 = (bf16[64,256,128]{2,1,0:T(8,128)(2,1)}, bf16[4,64,256]{2,1,0:T(8,128)(2,1)}) custom-call(bf16[64,256,128]{2,1,0:T(8,128)(2,1)} %get-tuple-element.31.z_ref, bf16[4,4,64,256]{3,2,1,0:T(8,128)(2,1)} %bitcast.84, s32[64,1,256]{2,1,0:T(1,128)} %broadcast_in_dim.14.mask_ref, bf16[2,128,512]{2,1,0:T(8,128)(2,1)} %wq_ref.14, ...), custom_call_target="tpu_custom_call" | custom-call | flops 49999998976 | bytes 16777216 | tf_op jit(solution)/shard_map/start_attention/pallas_call | solution.py:379
  865.8 6.9 copy.101
  872.7 5.0 all-to-all-start.2
  878.6 50.7 %all-gather.8 = bf16[16,64,256]{2,1,0:T(8,128)(2,1)} all-gather(bf16[4,64,256]{2,1,0:T(8,128)(2,1)S(1)} %copy-done.8), channel_id=10, replica_groups=mesh['req'=4,'dap'=4] {'dap'}, dimensions={0}, use_global_device_ids=true | all-gather | bytes 655360 | tf_op jit(solution)/shard_map/all_gather | solution.py:424
  932.9 6.9 copy.102
  939.8 139.5 %end_stage.2 = (bf16[256,64,128]{2,1,0:T(8,128)(2,1)}, bf16[8,64,256]{2,1,0:T(8,128)(2,1)}) custom-call(bf16[256,64,128]{2,1,0:T(8,128)(2,1)} %bitcast.74, bf16[4,4,64,256]{3,2,1,0:T(8,128)(2,1)} %bitcast.81, s32[64,1,256]{2,1,0:T(1,128)} %broadcast_in_dim.15.mask_ref, bf16[2,128,512]{2,1,0:T(8,128)(2,1)} %wq_ref.15, bf16[2,128,128]{2,1,0:T(8,128)(2,1)} %wo_ref.23, ...), custom_call_target="tpu_custom_call" | custom-call | flops 60000002048 | bytes 16777216 | tf_op jit(solution)/shard_map/end_stage/pallas_call | solution.py:414
  1081.1 14.4 all-gather.42.cloned.1.call-done
  1095.5 34.8 %row_attention.3 = bf16[16,256,256]{2,1,0:T(8,128)(2,1)} custom-call(bf16[16,256,256]{2,1,0:T(8,128)(2,1)} %bitcast.76, bf16[4,8,64,256]{3,2,1,0:T(8,128)(2,1)} %bitcast.104, s32[16,1,256]{2,1,0:T(1,128)} %broadcast_in_dim.12.mask_ref, bf16[2,256,1024]{2,1,0:T(8,128)(2,1)} %wq_ref.12, bf16[2,256,256]{2,1,0:T(8,128)(2,1)} %wo_ref.18), custom_call_target="tpu_custom_call" | custom-call | flops 40000000000 | bytes 16777216 | tf_op jit(solution)/shard_map/row_attention/pallas_call | solution.py:133
  1133.1 28.1 %all_to_all.126 = bf16[16,256,256]{2,0,1:T(8,128)(2,1)S(1)} all-to-all(bf16[16,256,256]{2,0,1:T(8,128)(2,1)S(1)} %copy.104), channel_id=1, replica_groups=mesh['req'=4,'dap'=4] {'dap'}, dimensions={1} | all-to-all | bytes 4194304 | tf_op jit(solution)/shard_map/all_to_all | solution.py:472
  1163.3 86.0 %column_stage.3 = (bf16[64,64,256]{2,1,0:T(8,128)(2,1)}, bf16[64,64,64]{2,1,0:T(8,128)(2,1)}) custom-call(bf16[64,64,256]{2,1,0:T(8,128)(2,1)} %bitcast.77, s32[64,1,64]{2,1,0:T(1,128)} %copy.92.mask_ref, bf16[2,256,1024]{2,1,0:T(8,128)(2,1)} %wq_ref.13, bf16[2,256,256]{2,1,0:T(8,128)(2,1)} %wo_ref.19, bf16[2,256,1024]{2,1,0:T(8,128)(2,1)} %wi_ref.6, ...), custom_call_target="tpu_custom_call" | custom-call | flops 40000000000 | bytes 16777216 | tf_op jit(solution)/shard_map/column_stage/pallas_call | solution.py:195
  1253.4 31.4 %all-gather.46.cloned.1.call-done = bf16[256,64,64]{2,0,1:T(8,128)(2,1)} async-done(((bf16[64,64,64]{2,0,1:T(8,128)(2,1)}), bf16[256,64,64]{2,0,1:T(8,128)(2,1)}) %all-gather.46.cloned.1.call-update) | async-done | bytes 2097168 | tf_op jit(solution)/shard_map/all_gather | solution.py:424
  1284.8 7.0 copy.109.left_ref
  1293.3 98.1 %all-gather.44.cloned.1.call-done = bf16[1024,64,128]{2,1,0:T(8,128)(2,1)} async-done(((bf16[256,64,128]{2,1,0:T(8,128)(2,1)}), bf16[1024,64,128]{2,1,0:T(8,128)(2,1)}) %all-gather.44.cloned.1.call-update) | async-done | bytes 16777232 | tf_op jit(solution)/shard_map/all_gather | solution.py:424
  1391.4 57.4 %outer_product.3.z_ref = bf16[128,256,128]{2,1,0:T(8,128)(2,1)} custom-call(s32[2]{0:T(128)} %pad_add_fusion.where_ref, bf16[4,256,64,128]{3,2,1,0:T(8,128)(2,1)} %bitcast.98, bf16[256,64,64]{2,1,0:T(8,128)(2,1)} %copy.109.left_ref, bf16[32,256,64]{2,1,0:T(8,128)(2,1)} %slice_bitcast_fusion.right_ref, bf16[256,64]{1,0:T(8,128)(2,1)} %copy.97.ml_ref, ...), custom_call_target="tpu_custom_call" | custom-call | flops 20000000000 | bytes 16777216 | tf_op jit(solution)/shard_map/outer_product/pallas_call | solution.py:239
  1448.8 66.2 %triangle_project.6 = (bf16[128,128,256]{2,1,0:T(8,128)(2,1)}, bf16[128,128,256]{2,1,0:T(8,128)(2,1)}) custom-call(s32[2]{0:T(128)} %pad_add_fusion.where_ref, bf16[128,256,128]{2,1,0:T(8,128)(2,1)} %outer_product.3.z_ref, f32[128,1,256]{2,1,0:T(1,128)} %convert_element_type.13.mask_ref, bf16[2,640,128]{2,1,0:T(8,128)(2,1)} %bitcast.87), custom_call_target="tpu_custom_call" | custom-call | flops 20000000000 | bytes 16777216 | tf_op jit(solution)/shard_map/triangle_project/pallas_call | solution.py:272
  1515.1 28.8 %all-gather.48.cloned.1.call-done = bf16[256,128,256]{2,1,0:T(8,128)(2,1)} async-done(((bf16[128,128,256]{2,1,0:T(8,128)(2,1)}), bf16[256,128,256]{2,1,0:T(8,128)(2,1)}) %all-gather.48.cloned.1.call-update) | async-done | bytes 16777232 | tf_op jit(solution)/shard_map/all_gather | solution.py:428
  1543.9 69.6 %triangle_out.3.z_ref = bf16[128,256,128]{2,1,0:T(8,128)(2,1)} custom-call(s32[2]{0:T(128)} %pad_add_fusion.where_ref, bf16[128,256,128]{2,1,0:T(8,128)(2,1)} %outer_product.3.z_ref, bf16[128,128,256]{2,1,0:T(8,128)(2,1)} %get-tuple-element.39.a_ref, bf16[2,128,128,256]{3,2,1,0:T(8,128)(2,1)} %bitcast.101, bf16[2,128,640]{2,1,0:T(8,128)(2,1)} %wp_ref.6, ...), custom_call_target="tpu_custom_call" | custom-call | flops 20000000000 | bytes 16777216 | tf_op jit(solution)/shard_map/triangle_out/pallas_call | solution.py:355
  1613.5 62.1 %triangle_project.7 = (bf16[128,128,128]{2,1,0:T(8,128)(2,1)}, bf16[128,128,256]{2,1,0:T(8,128)(2,1)}) custom-call(s32[2]{0:T(128)} %pad_add_fusion.where_ref, bf16[128,256,128]{2,1,0:T(8,128)(2,1)} %triangle_out.3.z_ref, f32[128,1,256]{2,1,0:T(1,128)} %convert_element_type.13.mask_ref, bf16[2,640,128]{2,1,0:T(8,128)(2,1)} %bitcast.89), custom_call_target="tpu_custom_call" | custom-call | flops 20000000000 | bytes 16777216 | tf_op jit(solution)/shard_map/triangle_project/pallas_call | solution.py:272
  1676.2 19.7 all-gather.50.cloned.1.call-done
  1695.9 31.3 %all-gather.52.cloned.1.call-done = bf16[256,128,256]{2,1,0:T(8,128)(2,1)} async-done(((bf16[128,128,256]{2,1,0:T(8,128)(2,1)}), bf16[256,128,256]{2,1,0:T(8,128)(2,1)}) %all-gather.52.cloned.1.call-update) | async-done | bytes 16777232 | tf_op jit(solution)/shard_map/all_gather | solution.py:428
  1727.2 63.0 %triangle_in.3 = (bf16[64,256,128]{2,1,0:T(8,128)(2,1)}, bf16[4,64,256]{2,1,0:T(8,128)(2,1)}) custom-call(s32[2]{0:T(128)} %pad_add_fusion.where_ref, bf16[128,256,128]{2,1,0:T(8,128)(2,1)} %triangle_out.3.z_ref, bf16[2,128,128,128]{3,2,1,0:T(8,128)(2,1)} %bitcast.103, bf16[2,128,128,256]{3,2,1,0:T(8,128)(2,1)} %bitcast.99, bf16[2,128,640]{2,1,0:T(8,128)(2,1)} %wp_ref.7, ...), custom_call_target="tpu_custom_call" | custom-call | flops 20000000000 | bytes 16777216 | tf_op jit(solution)/shard_map/triangle_in/pallas_call | solution.py:355
  1790.2 8.9 all-gather.15
  1799.1 110.8 %start_attention.3 = (bf16[64,256,128]{2,1,0:T(8,128)(2,1)}, bf16[4,64,256]{2,1,0:T(8,128)(2,1)}) custom-call(bf16[64,256,128]{2,1,0:T(8,128)(2,1)} %get-tuple-element.43.z_ref, bf16[4,4,64,256]{3,2,1,0:T(8,128)(2,1)} %bitcast.83, s32[64,1,256]{2,1,0:T(1,128)} %broadcast_in_dim.14.mask_ref, bf16[2,128,512]{2,1,0:T(8,128)(2,1)} %wq_ref.14, ...), custom_call_target="tpu_custom_call" | custom-call | flops 49999998976 | bytes 16777216 | tf_op jit(solution)/shard_map/start_attention/pallas_call | solution.py:379
  1909.9 6.9 copy.112
  1916.8 5.0 all-to-all-start.5
  1921.8 51.5 %all-gather.16 = bf16[16,64,256]{2,1,0:T(8,128)(2,1)} all-gather(bf16[4,64,256]{2,1,0:T(8,128)(2,1)S(1)} %copy-done.9), channel_id=18, replica_groups=mesh['req'=4,'dap'=4] {'dap'}, dimensions={0}, use_global_device_ids=true | all-gather | bytes 655360 | tf_op jit(solution)/shard_map/all_gather | solution.py:424
  1977.0 6.9 copy.113
  1983.9 139.5 %end_stage.3 = (bf16[256,64,128]{2,1,0:T(8,128)(2,1)}, bf16[8,64,256]{2,1,0:T(8,128)(2,1)}) custom-call(bf16[256,64,128]{2,1,0:T(8,128)(2,1)} %bitcast.73, bf16[4,4,64,256]{3,2,1,0:T(8,128)(2,1)} %bitcast.82, s32[64,1,256]{2,1,0:T(1,128)} %broadcast_in_dim.15.mask_ref, bf16[2,128,512]{2,1,0:T(8,128)(2,1)} %wq_ref.15, bf16[2,128,128]{2,1,0:T(8,128)(2,1)} %wo_ref.23, ...), custom_call_target="tpu_custom_call" | custom-call | flops 60000002048 | bytes 16777216 | tf_op jit(solution)/shard_map/end_stage/pallas_call | solution.py:414
  2129.8 46.4 %all-to-all-done.6 = bf16[256,64,128]{2,1,0:T(8,128)(2,1)} async-done(((bf16[256,64,128]{2,1,0:T(8,128)(2,1)}), bf16[256,64,128]{2,1,0:T(8,128)(2,1)}, u32[]{:S(2)}, u32[]{:S(2)}) %all-to-all-start.6) | async-done | bytes 4194336 | tf_op jit(solution)/shard_map/all_to_all | solution.py:486
  2176.2 5.6 copy.114
  (88 shorter events, 53.5 us)
Async XLA Ops:
  7.2 22.4 %copy-start.10 = (s32[16,256]{1,0:T(8,128)S(1)}, s32[16,256]{1,0:T(8,128)}, u32[]{:S(2)}) copy-start(s32[16,256]{1,0:T(8,128)} %param.27) | copy-start | bytes 49156
  7.2 39.9 %all-gather.30.cloned.1.call-start = ((), (), s32[]{:S(2)}) async-start(), calls=%async_computation.7 | async-start | bytes 1310720 | tf_op jit(solution)/shard_map/all_gather | solution.py:424
  85.5 31.0 %all-to-all-start = ((bf16[16,256,256]{2,0,1:T(8,128)(2,1)}), bf16[16,256,256]{2,0,1:T(8,128)(2,1)S(1)}, u32[]{:S(2)}, u32[]{:S(2)}) async-start(bf16[16,256,256]{2,0,1:T(8,128)(2,1)} %copy.90), calls=%async_computation | async-start | bytes 4194304 | tf_op jit(solution)/shard_map/all_to_all | solution.py:472
  89.1 151.0 %all-gather.34.cloned.1.call-start = ((), (), s32[]{:S(2)}) async-start(), calls=%async_computation.9 | async-start | bytes 5242880 | tf_op jit(solution)/shard_map/all_gather | solution.py:424
  204.6 5.2 copy-start.7
  204.6 13.0 copy-start.5
  204.6 13.8 copy-start.4
  207.6 139.2 %all-gather.32.cloned.1.call-start = ((), (), s32[]{:S(2)}) async-start(), calls=%async_computation.8 | async-start | bytes 20971520 | tf_op jit(solution)/shard_map/all_gather | solution.py:424
  208.3 291.2 %all-gather.36.cloned.1.call-start = ((), (), s32[]{:S(2)}) async-start(), calls=%async_computation.10 | async-start | bytes 25165824 | tf_op jit(solution)/shard_map/all_gather | solution.py:428
  216.0 0.7 copy-start.2
  240.1 7.1 copy-start
  470.6 1.0 copy-start.6
  470.6 181.2 %all-gather.38.cloned.1.call-start = ((), (), s32[]{:S(2)}) async-start(), calls=%async_computation.11 | async-start | bytes 12582912 | tf_op jit(solution)/shard_map/all_gather | solution.py:428
  631.5 51.6 %all-gather.40.cloned.1.call-start = ((), (), s32[]{:S(2)}) async-start(), calls=%async_computation.12 | async-start | bytes 25165824 | tf_op jit(solution)/shard_map/all_gather | solution.py:428
  631.6 1.2 copy-start.11
  631.6 1.8 copy-start.12
  872.7 5.0 copy-start.3
  872.7 5.9 copy-start.8
  872.7 56.6 %all-to-all-start.2 = ((bf16[64,256,128]{2,0,1:T(8,128)(2,1)}), bf16[64,256,128]{2,0,1:T(8,128)(2,1)}, u32[]{:S(2)}, u32[]{:S(2)}) async-start(bf16[64,256,128]{2,0,1:T(8,128)(2,1)} %copy.101), calls=%async_computation.2 | async-start | bytes 8388608 | tf_op jit(solution)/shard_map/all_to_all | solution.py:484
  929.3 150.4 %all-to-all-start.1 = ((bf16[64,64,256]{2,1,0:T(8,128)(2,1)}), bf16[64,64,256]{2,1,0:T(8,128)(2,1)S(1)}, u32[]{:S(2)}, u32[]{:S(2)}) async-start(bf16[64,64,256]{2,1,0:T(8,128)(2,1)} %get-tuple-element.25), calls=%async_computation.1 | async-start | bytes 4194304 | tf_op jit(solution)/shard_map/all_to_all | solution.py:476
  932.9 162.7 %all-gather.42.cloned.1.call-start = ((), (), s32[]{:S(2)}) async-start(), calls=%async_computation.13 | async-start | bytes 1310720 | tf_op jit(solution)/shard_map/all_gather | solution.py:424
  1079.4 205.4 %all-gather.46.cloned.1.call-start = ((), (), s32[]{:S(2)}) async-start(), calls=%async_computation.15 | async-start | bytes 5242880 | tf_op jit(solution)/shard_map/all_gather | solution.py:424
  1252.2 139.2 %all-gather.44.cloned.1.call-start = ((), (), s32[]{:S(2)}) async-start(), calls=%async_computation.14 | async-start | bytes 20971520 | tf_op jit(solution)/shard_map/all_gather | solution.py:424
  1252.9 291.0 %all-gather.48.cloned.1.call-start = ((), (), s32[]{:S(2)}) async-start(), calls=%async_computation.16 | async-start | bytes 25165824 | tf_op jit(solution)/shard_map/all_gather | solution.py:428
  1284.8 7.1 copy-start.1
  1515.1 180.9 %all-gather.50.cloned.1.call-start = ((), (), s32[]{:S(2)}) async-start(), calls=%async_computation.17 | async-start | bytes 12582912 | tf_op jit(solution)/shard_map/all_gather | solution.py:428
  1675.7 51.6 %all-gather.52.cloned.1.call-start = ((), (), s32[]{:S(2)}) async-start(), calls=%async_computation.18 | async-start | bytes 25165824 | tf_op jit(solution)/shard_map/all_gather | solution.py:428
  1916.8 5.0 copy-start.9
  1916.8 56.6 %all-to-all-start.5 = ((bf16[64,256,128]{2,0,1:T(8,128)(2,1)}), bf16[64,256,128]{2,0,1:T(8,128)(2,1)}, u32[]{:S(2)}, u32[]{:S(2)}) async-start(bf16[64,256,128]{2,0,1:T(8,128)(2,1)} %copy.112), calls=%async_computation.5 | async-start | bytes 8388608 | tf_op jit(solution)/shard_map/all_to_all | solution.py:484
  1973.4 150.0 %all-to-all-start.4 = ((bf16[64,64,256]{2,1,0:T(8,128)(2,1)}), bf16[64,64,256]{2,1,0:T(8,128)(2,1)S(1)}, u32[]{:S(2)}, u32[]{:S(2)}) async-start(bf16[64,64,256]{2,1,0:T(8,128)(2,1)} %get-tuple-element.36), calls=%async_computation.4 | async-start | bytes 4194304 | tf_op jit(solution)/shard_map/all_to_all | solution.py:476
  2123.4 52.8 %all-to-all-start.6 = ((bf16[256,64,128]{2,1,0:T(8,128)(2,1)}), bf16[256,64,128]{2,1,0:T(8,128)(2,1)}, u32[]{:S(2)}, u32[]{:S(2)}) async-start(bf16[256,64,128]{2,1,0:T(8,128)(2,1)} %get-tuple-element.47), calls=%async_computation.6 | async-start | bytes 8388608 | tf_op jit(solution)/shard_map/all_to_all | solution.py:486
Sparse Core Ops, SparseCore 0:
  29.6 17.4 all-gather.29
  207.7 32.4 all-gather.33
  241.7 105.0 all-gather.31
  470.8 28.7 all-gather.35
  631.7 20.1 all-gather.37
  653.2 29.8 all-gather.39
  1079.5 15.9 all-gather.41
  1252.3 32.3 all-gather.45
  1286.3 105.0 all-gather.43
  1515.2 28.7 all-gather.47
  1675.8 20.0 all-gather.49
  1697.3 29.8 all-gather.51
